TPU v7x, 32 devices: a whole 2x2x4 slice. The times are simulated.
32 devices in a mesh: task: 2 (over x), batch: 16 (over z, y, core).
Axes of the slice: x: 2, y: 2, z: 4, core: 2. Of those that a mesh axis runs over, the one named last changes fastest.
Arguments:
- pooled: bfloat16 [12288, 3328], P('batch'), may hold values from -6 to 6
- gate_weight: bfloat16 [3328, 8, 4], P(None, 'task'), may hold values from -0.21875 to 0.21875
- w_first: bfloat16 [8, 3328, 1024], P('task', 'batch'), may hold values from -0.15625 to 0.15625
- w_second: bfloat16 [8, 1024, 512], P('task', 'batch'), may hold values from -0.25 to 0.25
- w_third: bfloat16 [8, 512, 256], P('task', 'batch'), may hold values from -0.375 to 0.375
- tower_hidden: bfloat16 [4, 256, 128], P('task'), may hold values from -0.5 to 0.5
- tower_out: bfloat16 [4, 128], P('task'), may hold values from -0.75 to 0.75
Outputs:
- task_logits: float32 [12288, 4], P('batch', 'task')
All inputs are finite; a program needn't handle non-finite values.
Results may differ from a plain program's by a relative error of at most 0.02.
Values may be sent and summed in bfloat16 or wider, within the bound.
A program may use at most 128 MiB of HBM per device.

v0:
```python
import jax
import jax.numpy as jnp
from jax import lax
from jax.sharding import PartitionSpec as P


def per_device(pooled, gate_weight, w_first, w_second, w_third, tower_hidden, tower_out):
    tok_rows = pooled.shape[0]
    width_in = pooled.shape[1]
    local_experts = w_first.shape[0]
    all_tasks = gate_weight.shape[2]
    own_tasks = tower_hidden.shape[0]
    gathered = lax.all_gather(w_first, "batch", axis=1, tiled=True)
    deep_rows, deep_width = (w_second.shape[1], w_second.shape[2])
    last_rows, last_width = (w_third.shape[1], w_third.shape[2])
    halves = deep_width // last_width
    packed = jnp.concatenate(
        [w_second[:, :, i * last_width : (i + 1) * last_width] for i in range(halves)] + [w_third],
        axis=1,
    )
    gathered, packed = lax.optimization_barrier((gathered, packed))
    packed = lax.all_gather(packed, "batch", axis=1, tiled=False)
    second_all = jnp.concatenate(
        [packed[:, :, i * deep_rows : (i + 1) * deep_rows] for i in range(halves)], axis=3
    ).reshape(local_experts, -1, deep_width)
    third_all = packed[:, :, halves * deep_rows :].reshape(local_experts, -1, last_width)
    summed = jnp.einsum("tr,erh->eth", pooled, gathered, preferred_element_type=jnp.float32)
    first = jax.nn.relu(summed).astype(jnp.bfloat16)
    logits = jnp.dot(
        pooled,
        gate_weight.reshape(width_in, local_experts * all_tasks),
        preferred_element_type=jnp.float32,
    )
    weights = jnp.exp(logits.reshape(tok_rows, local_experts, all_tasks))
    gate_total = jnp.sum(weights, axis=1)
    columns = first
    second = jax.nn.relu(
        jnp.einsum("etr,erh->eth", columns, second_all, preferred_element_type=jnp.float32)
    ).astype(jnp.bfloat16)
    columns = second
    expert_out = jax.nn.relu(
        jnp.einsum("etr,erh->eth", columns, third_all, preferred_element_type=jnp.float32)
    ).astype(jnp.bfloat16)
    numer = jnp.einsum("tek,eth->tkh", weights, expert_out.astype(jnp.float32))
    groups = all_tasks // own_tasks
    me = lax.axis_index("task")
    numer_own = lax.dynamic_slice_in_dim(numer, me * own_tasks, own_tasks, 1)
    total_own = lax.dynamic_slice_in_dim(gate_total, me * own_tasks, own_tasks, 1)
    for shift in range(1, groups):
        ring = [(i, (i + shift) % groups) for i in range(groups)]
        other = lax.rem(me + shift, groups) * own_tasks
        numer_sent = lax.dynamic_slice_in_dim(numer, other, own_tasks, 1).astype(jnp.bfloat16)
        total_sent = lax.dynamic_slice_in_dim(gate_total, other, own_tasks, 1)
        numer_own = numer_own + lax.ppermute(numer_sent, "task", ring).astype(jnp.float32)
        total_own = total_own + lax.ppermute(total_sent, "task", ring)
    mix = (numer_own / total_own[:, :, None]).astype(jnp.bfloat16)
    tower = jax.nn.relu(
        jnp.einsum("tkh,khm->tkm", mix, tower_hidden, preferred_element_type=jnp.float32)
    ).astype(jnp.bfloat16)
    return jnp.einsum("tkm,km->tk", tower, tower_out, preferred_element_type=jnp.float32)


def solution(mesh):
    placed = (
        P("batch", None),
        P(None, "task", None),
        P("task", "batch", None),
        P("task", "batch", None),
        P("task", "batch", None),
        P("task", None, None),
        P("task", None),
    )
    return jax.shard_map(
        per_device, mesh=mesh, in_specs=placed, out_specs=P("batch", "task"), check_vma=False
    )
```

profile of v0, /device:TPU:0, one launch (start us, length us, event | category | flops | bytes accessed | tf_op | source)
XLA Modules:
  0.0 290.8 jit_solution(5870801982256246528)
XLA Ops:
  6.5 0.0 copy-start
  6.5 0.0 all-gather.4.cloned.1.call-start
  6.5 0.7 all-gather.4.cloned.1.call-update
  7.3 0.0 all-gather.6.cloned.1.call-start
  7.3 1.0 fusion.32
  8.3 1.6 pad_maximum_fusion.1
  9.9 140.2 %all-gather.4.cloned.1.call-done = bf16[4,3328,1024]{2,1,0:T(8,128)(2,1)} async-done(((bf16[4,208,1024]{2,1,0:T(8,128)(2,1)}), bf16[4,3328,1024]{2,1,0:T(8,128)(2,1)}) %all-gather.4.cloned.1.call-update) | async-done | bytes 27262992 | tf_op jit(solution)/shard_map/all_gather | solution.py:13
  150.1 0.0 all-gather.6.cloned.1.call-update
  150.1 0.9 reshape.12
  151.0 4.1 %fusion.33 = (f32[768,4]{0,1:T(4,128)S(1)}, bf16[768,4,4]{0,2,1:T(4,128)(2,1)S(1)}) fusion(bf16[4,4,3328]{2,1,0:T(4,128)(2,1)S(1)} %dot_general.26, bf16[768,3328]{1,0:T(8,128)(2,1)} %param.7), kind=kOutput, calls=%fused_computation.36 | convolution fusion | flops 81810432 | bytes 5255168 | tf_op jit(solution)/shard_map/dot_general | solution.py:29
  155.1 1.3 copy.9
  156.4 51.7 %all-gather.6.cloned.1.call-done = bf16[4,2560,256]{2,1,0:T(8,128)(2,1)} async-done(((bf16[4,160,256]{2,1,0:T(8,128)(2,1)}), bf16[4,2560,256]{2,1,0:T(8,128)(2,1)}) %all-gather.6.cloned.1.call-update) | async-done | bytes 5242896 | tf_op jit(solution)/shard_map/all_gather | solution.py:22
  208.1 1.3 slice.22
  209.4 2.8 fusion.31
  212.2 2.5 pad_maximum_fusion
  214.7 36.6 %fusion = bf16[4,768,512]{2,1,0:T(8,128)(2,1)} fusion(bf16[4,1024,512]{2,1,0:T(8,128)(2,1)} %bitcast.37, bf16[4,3328,1024]{2,1,0:T(8,128)(2,1)} %all-gather.4.cloned.1.call-done, bf16[768,3328]{1,0:T(8,128)(2,1)} %param.7), kind=kOutput, calls=%fused_computation.1 | convolution fusion | flops 24165482496 | bytes 39714816 | tf_op jit(solution)/shard_map/etr,erh->eth/dot_general | solution.py:38
  251.3 0.0 copy-start.1
  251.3 2.9 %fusion.10 = bf16[4,768,256]{2,1,0:T(8,128)(2,1)S(1)} fusion(bf16[4,512,256]{2,1,0:T(8,128)(2,1)S(1)} %bitcast.38, bf16[4,768,512]{2,1,0:T(8,128)(2,1)} %fusion), kind=kOutput, calls=%fused_computation.9 | convolution fusion | flops 810024960 | bytes 5767168 | tf_op jit(solution)/shard_map/etr,erh->eth/dot_general | solution.py:42
  254.2 0.0 copy-done.1
  254.2 1.5 fusion.13
  255.8 0.0 copy-start.2
  255.8 1.6 dynamic-slice_convert_fusion
  257.4 1.5 collective-permute-start
  258.9 0.6 collective-permute-start.1
  259.4 18.0 %collective-permute-done.1 = f32[768,2]{0,1:T(2,128)S(1)} collective-permute-done((f32[768,2]{0,1:T(2,128)S(1)}, f32[768,2]{0,1:T(2,128)S(1)}, u32[]{:S(2)}, u32[]{:S(2)}) %collective-permute-start.1) | collective-permute-done | bytes 6176 | tf_op jit(solution)/shard_map/ppermute | solution.py:55
  277.5 0.9 copy.10
  278.4 0.0 collective-permute-done
  278.4 3.2 %fusion.16 = bf16[768,2,256]{2,1,0:T(2,128)(2,1)} fusion(bf16[768,2,256]{2,1,0:T(2,128)(2,1)} %collective-permute-done, f32[768,4,256]{2,1,0:T(4,128)S(1)} %fusion.13, s32[]{:T(128)S(6)} %select_n.8, f32[768,2]{1,0:T(8,128)} %copy.10), kind=kLoop, calls=%fused_computation.17 | loop fusion | flops 1572864 | bytes 3151876 | tf_op jit(solution)/shard_map/convert_element_type | solution.py:56
  281.7 0.0 copy-done
  281.7 0.0 copy-done.2
  281.7 1.6 fusion.19
  283.3 0.6 copy.25
  (3 shorter events, 0.0 us)
Async XLA Ops:
  6.5 275.1 %copy-start = (bf16[2,256,128]{2,1,0:T(8,128)(2,1)S(1)}, bf16[2,256,128]{2,1,0:T(8,128)(2,1)}, u32[]{:S(2)}) copy-start(bf16[2,256,128]{2,1,0:T(8,128)(2,1)} %param.12) | copy-start | bytes 393220
  6.5 143.5 %all-gather.4.cloned.1.call-start = ((), (), s32[]{:S(2)}) async-start(), calls=%async_computation | async-start | bytes 28966912 | tf_op jit(solution)/shard_map/all_gather | solution.py:13
  7.3 200.9 %all-gather.6.cloned.1.call-start = ((), (), s32[]{:S(2)}) async-start(), calls=%async_computation.1 | async-start | bytes 5570560 | tf_op jit(solution)/shard_map/all_gather | solution.py:22
  251.3 3.0 %copy-start.1 = (bf16[768,4,4]{1,2,0:T(4,128)(2,1)S(1)}, bf16[768,4,4]{1,2,0:T(4,128)(2,1)}, u32[]{:S(2)}) copy-start(bf16[768,4,4]{1,2,0:T(4,128)(2,1)} %copy.9) | copy-start | bytes 73732
  255.8 25.9 %copy-start.2 = (bf16[2,128]{1,0:T(2,128)(2,1)S(1)}, bf16[2,128]{1,0:T(2,128)(2,1)}, u32[]{:S(2)}) copy-start(bf16[2,128]{1,0:T(2,128)(2,1)} %param.13) | copy-start | bytes 1540
  257.4 21.0 %collective-permute-start = (bf16[768,2,256]{2,1,0:T(2,128)(2,1)}, bf16[768,2,256]{2,1,0:T(2,128)(2,1)}, u32[]{:S(2)}, u32[]{:S(2)}) collective-permute-start(bf16[768,2,256]{2,1,0:T(2,128)(2,1)} %dynamic-slice_convert_fusion), channel_id=1, source_target_pairs={{0,16},{16,0},{1,17},{17,1},{2,18},{18,2},{3,19},{19,3},{4,20},{20... | collective-permute-start | bytes 2359304 | tf_op jit(solution)/shard_map/ppermute | solution.py:54
  258.9 18.6 %collective-permute-start.1 = (f32[768,2]{0,1:T(2,128)S(1)}, f32[768,2]{0,1:T(2,128)S(1)}, u32[]{:S(2)}, u32[]{:S(2)}) collective-permute-start(f32[768,2]{0,1:T(2,128)S(1)} %constant_dynamic-slice_fusion), channel_id=1, source_target_pairs={{0,16},{16,0},{1,17},{17,1},{2,18},{18,2},{3,19},{19,3},{4,20},{20... | collective-permute-start | bytes 18440 | tf_op jit(solution)/shard_map/ppermute | solution.py:55
Sparse Core Ops, SparseCore 0:
  8.9 141.1 all-gather.3
  152.3 55.7 all-gather.5
where the time goes:
time: 291 us
  waiting for transfers between devices  211 us (73%)
  matrix products  46.7 us (16%)
  between operations  13.5 us (5%)
  local copies, waits for them, and re-layouts  10.6 us (4%)
  other arithmetic  7.28 us (3%)
    all_gather x1, waiting for transfers between devices, per_device(): gathered = lax.all_gather(w_first, 'batch', axis=1, tiled=True)  140 us
    all_gather x1, waiting for transfers between devices, per_device(): packed = lax.all_gather(packed, 'batch', axis=1, tiled=False)  51.7 us
    dot_general x1, matrix products, per_device(): jnp.einsum('etr,erh->eth', columns, second_all, preferred_element_type=jn...  36.6 us
    ppermute x1, waiting for transfers between devices, per_device(): total_own = total_own + lax.ppermute(total_sent, 'task', ring)  18 us
  transfers between devices with their start and end apart: 4, of which 3 were waited for; matrix products, arithmetic and copies ran while one was open for 3% of the time, Pallas kernels for 0%

commit v1 on v0

--- a/solution.py
+++ b/solution.py
@@ -10,7 +10,8 @@
     local_experts = w_first.shape[0]
     all_tasks = gate_weight.shape[2]
     own_tasks = tower_hidden.shape[0]
-    gathered = lax.all_gather(w_first, "batch", axis=1, tiled=True)
+    shards = lax.all_gather(w_first, "batch", axis=0, tiled=False)
+    gathered = jnp.concatenate(shards, axis=1)
     deep_rows, deep_width = (w_second.shape[1], w_second.shape[2])
     last_rows, last_width = (w_third.shape[1], w_third.shape[2])
     halves = deep_width // last_width

time: 291 us -> 306 us (1.052)
  local copies, waits for them, and re-layouts: 10.6 us -> 29.6 us
  other arithmetic: 7.28 us -> 4.08 us
    reshape x0 -> x1, local copies, waits for them, and re-layouts: none -> 18.9 us  [per_device(): gathered = jnp.concatenate(shards, axis=1)]
    convert_element_type x1 -> x0, other arithmetic: 3.22 us -> none  [per_device(): mix = (numer_own / total_own[:, :, None]).astype(jnp.bfloat16)]
where the time goes in v1:
time: 306 us
  waiting for transfers between devices  209 us (68%)
  matrix products  47.2 us (15%)
  local copies, waits for them, and re-layouts  29.6 us (10%)
  between operations  13.5 us (4%)
  other arithmetic  4.08 us (1%)
    all_gather x1, waiting for transfers between devices, per_device(): shards = lax.all_gather(w_first, 'batch', axis=0, tiled=False)  140 us
    all_gather x1, waiting for transfers between devices, per_device(): packed = lax.all_gather(packed, 'batch', axis=1, tiled=False)  50.4 us
    dot_general x1, matrix products, per_device(): jnp.einsum('etr,erh->eth', columns, second_all, preferred_element_type=jn...  36.6 us
    reshape x1, local copies, waits for them, and re-layouts, per_device(): gathered = jnp.concatenate(shards, axis=1)  18.9 us
    ppermute x1, waiting for transfers between devices, per_device(): total_own = total_own + lax.ppermute(total_sent, 'task', ring)  18 us
  transfers between devices with their start and end apart: 4, of which 3 were waited for; matrix products, arithmetic and copies ran while one was open for 3% of the time, Pallas kernels for 0%

profile of v1, /device:TPU:0, one launch (start us, length us, event | category | flops | bytes accessed | tf_op | source)
XLA Modules:
  0.0 305.9 jit_solution(2440761249411336292)
XLA Ops:
  6.5 0.0 copy-start
  6.5 0.0 all-gather.5.cloned.1.call-start
  6.5 0.7 all-gather.5.cloned.1.call-update
  7.3 0.0 all-gather.7.cloned.1.call-start
  7.3 1.0 fusion.30
  8.3 1.6 pad_maximum_fusion.1
  9.9 140.2 %all-gather.5.cloned.1.call-done = bf16[64,208,1024]{2,1,0:T(8,128)(2,1)} async-done(((bf16[4,208,1024]{2,1,0:T(8,128)(2,1)}), bf16[64,208,1024]{2,1,0:T(8,128)(2,1)}) %all-gather.5.cloned.1.call-update) | async-done | bytes 27262992 | tf_op jit(solution)/shard_map/all_gather | solution.py:13
  150.1 0.0 copy-start.2
  150.1 18.9 %copy.23 = bf16[4,16,208,1024]{3,2,1,0:T(8,128)(2,1)} copy(bf16[4,16,208,1024]{3,2,0,1:T(8,128)(2,1)} %bitcast.40) | data formatting | bytes 54525952 | tf_op jit(solution)/shard_map/reshape | solution.py:14
  169.0 0.0 all-gather.7.cloned.1.call-update
  169.1 0.0 copy-done.2
  169.2 4.1 %fusion.31 = (f32[768,4]{0,1:T(4,128)S(1)}, bf16[768,4,4]{0,2,1:T(4,128)(2,1)S(1)}) fusion(bf16[4,4,3328]{2,1,0:T(4,128)(2,1)S(1)} %dot_general.26, bf16[768,3328]{1,0:T(8,128)(2,1)} %param.7), kind=kOutput, calls=%fused_computation.36 | convolution fusion | flops 81810432 | bytes 5255168 | tf_op jit(solution)/shard_map/dot_general | solution.py:30
  173.2 1.3 copy.26
  174.5 50.4 %all-gather.7.cloned.1.call-done = bf16[4,2560,256]{2,1,0:T(8,128)(2,1)} async-done(((bf16[4,160,256]{2,1,0:T(8,128)(2,1)}), bf16[4,2560,256]{2,1,0:T(8,128)(2,1)}) %all-gather.7.cloned.1.call-update) | async-done | bytes 5242896 | tf_op jit(solution)/shard_map/all_gather | solution.py:23
  225.0 1.3 slice.22
  226.3 2.8 fusion.29
  229.1 2.5 pad_maximum_fusion
  231.5 36.6 %fusion = bf16[4,768,512]{2,1,0:T(8,128)(2,1)} fusion(bf16[4,1024,512]{2,1,0:T(8,128)(2,1)} %bitcast.43, bf16[4,3328,1024]{2,1,0:T(8,128)(2,1)} %bitcast.39, bf16[768,3328]{1,0:T(8,128)(2,1)} %param.7), kind=kOutput, calls=%fused_computation.1 | convolution fusion | flops 24165482496 | bytes 39714816 | tf_op jit(solution)/shard_map/etr,erh->eth/dot_general | solution.py:39
  268.1 2.9 maximum_convert_fusion.4
  271.1 0.0 copy-done.1
  271.1 1.5 fusion.14
  272.6 0.7 constant_dynamic-slice_fusion.1
  273.3 1.0 copy.49
  274.3 1.5 collective-permute-start
  275.8 0.6 collective-permute-start.1
  276.3 18.0 %collective-permute-done.1 = f32[768,2]{0,1:T(2,128)S(1)} collective-permute-done((f32[768,2]{0,1:T(2,128)S(1)}, f32[768,2]{0,1:T(2,128)S(1)}, u32[]{:S(2)}, u32[]{:S(2)}) %collective-permute-start.1) | collective-permute-done | bytes 6176 | tf_op jit(solution)/shard_map/ppermute | solution.py:56
  294.4 1.8 constant_dynamic-slice_fusion.2
  296.2 0.0 collective-permute-done
  296.2 0.0 copy-done
  296.2 0.0 copy-done.3
  296.3 2.2 fusion.18
  298.4 0.6 copy.50
  (6 shorter events, 0.1 us)
Async XLA Ops:
  6.5 289.7 %copy-start = (bf16[2,256,128]{2,1,0:T(8,128)(2,1)S(1)}, bf16[2,256,128]{2,1,0:T(8,128)(2,1)}, u32[]{:S(2)}) copy-start(bf16[2,256,128]{2,1,0:T(8,128)(2,1)} %param.12) | copy-start | bytes 393220
  6.5 143.6 %all-gather.5.cloned.1.call-start = ((), (), s32[]{:S(2)}) async-start(), calls=%async_computation | async-start | bytes 28966912 | tf_op jit(solution)/shard_map/all_gather | solution.py:13
  7.3 217.7 %all-gather.7.cloned.1.call-start = ((), (), s32[]{:S(2)}) async-start(), calls=%async_computation.1 | async-start | bytes 5570560 | tf_op jit(solution)/shard_map/all_gather | solution.py:23
  150.1 19.0 %copy-start.2 = (bf16[3328,4,4]{0,2,1:T(4,128)(2,1)S(1)}, bf16[3328,4,4]{0,2,1:T(4,128)(2,1)}, u32[]{:S(2)}) copy-start(bf16[3328,4,4]{0,2,1:T(4,128)(2,1)} %param.8) | copy-start | bytes 319492
  268.1 3.0 copy-start.1
  272.6 23.7 %copy-start.3 = (bf16[2,128]{1,0:T(2,128)(2,1)S(1)}, bf16[2,128]{1,0:T(2,128)(2,1)}, u32[]{:S(2)}) copy-start(bf16[2,128]{1,0:T(2,128)(2,1)} %param.13) | copy-start | bytes 1540
  274.3 21.9 %collective-permute-start = (bf16[768,2,256]{2,0,1:T(8,128)(2,1)}, bf16[768,2,256]{2,0,1:T(8,128)(2,1)}, u32[]{:S(2)}, u32[]{:S(2)}) collective-permute-start(bf16[768,2,256]{2,0,1:T(8,128)(2,1)} %copy.49), channel_id=1, source_target_pairs={{0,16},{16,0},{1,17},{17,1},{2,18},{18,2},{3,19},{19,3},{4,20},{20... | collective-permute-start | bytes 2359304 | tf_op jit(solution)/shard_map/ppermute | solution.py:55
  275.8 18.6 %collective-permute-start.1 = (f32[768,2]{0,1:T(2,128)S(1)}, f32[768,2]{0,1:T(2,128)S(1)}, u32[]{:S(2)}, u32[]{:S(2)}) collective-permute-start(f32[768,2]{0,1:T(2,128)S(1)} %constant_dynamic-slice_fusion), channel_id=1, source_target_pairs={{0,16},{16,0},{1,17},{17,1},{2,18},{18,2},{3,19},{19,3},{4,20},{20... | collective-permute-start | bytes 18440 | tf_op jit(solution)/shard_map/ppermute | solution.py:56
Sparse Core Ops, SparseCore 0:
  8.9 141.1 all-gather.4
  169.2 55.7 all-gather.6
